TPU v7x, 32 devices: a whole 2x2x4 slice. The times are simulated.
32 devices in a mesh: seq: 8 (over z, x), batch: 4 (over y, core).
Axes of the slice: x: 2, y: 2, z: 4, core: 2. Of those that a mesh axis runs over, the one named last changes fastest.
Arguments:
- hidden: bfloat16 [8, 2048, 4096], P('batch', None, 'seq')
- gain: float32 [4096], P('seq'), may hold values from 0.5 to 1.5
- value_weight: float32 [4096], P('seq'), may hold values from -0.09375 to 0.09375
- rewards: float32 [8, 2048], P('batch', 'seq'), may hold values from -1.5 to 1.5
- reward_mask: int32 [8, 2048], P('batch', 'seq'), may hold values 0 or 1
- lengths: int32 [8], P('batch'), may hold values from 512 to 2048
- horizon: float32 [8], P('batch'), may hold values from 24 to 16384
Outputs:
- advantages: float32 [8, 2048], P(None, ('seq', 'batch'))
- returns: float32 [8, 2048], P(None, ('seq', 'batch'))
All inputs are finite; a program needn't handle non-finite values. No bound on the sum of `reward_mask` on one device may be relied on, other than what follows from the above.
Results may differ from a plain program's by a relative error of at most 0.0003.
Values may be sent and summed in bfloat16 or wider, within the bound.
A program may use at most 64 MiB of HBM per device.

v0:
```python
import jax
import jax.numpy as jnp
from jax import lax
from jax.sharding import PartitionSpec as P

D = 4096
EPS = 1e-05


def from_behind(value, axis, steps):
    count = lax.axis_size(axis)
    initial, last = (max(0, -steps), min(count, count - steps))
    return lax.ppermute(value, axis, [(source, source + steps) for source in range(initial, last)])


def entering(array, axis, combine, identity):
    devices, position = (lax.axis_size(axis), lax.axis_index(axis))
    everything = jax.tree.map(lambda part: lax.all_gather(part, axis), array)
    start = jax.tree.map(
        lambda part, zero: jnp.broadcast_to(jnp.asarray(zero, part.dtype), part.shape),
        array,
        identity,
    )

    def step(k, before):
        at = devices - 1 - k
        reached = at > position
        new = combine(before, jax.tree.map(lambda part: part[at], everything))
        return jax.tree.map(lambda a, b: jnp.where(reached, a, b), new, before)

    return lax.fori_loop(0, devices, step, start)


def per_device(hidden, gain, value_weight, rewards, reward_mask, lengths, horizon):
    my_index = lax.axis_index("seq")
    block = rewards.shape[1]
    wide_rows = hidden.astype(jnp.float32)
    part_squares = jnp.sum(wide_rows * wide_rows, -1)
    part_projected = jnp.sum(wide_rows * (gain * value_weight), -1)
    squares, projected = (
        lax.psum_scatter(part_squares, "seq", scatter_dimension=1, tiled=True),
        lax.psum_scatter(part_projected, "seq", scatter_dimension=1, tiled=True),
    )
    values = projected * lax.rsqrt(squares / D + EPS)
    positions = my_index * block + jnp.arange(block, dtype=jnp.int32)
    valid = (positions[None, :] < lengths[:, None]).astype(jnp.float32)
    next_valid = (positions[None, :] + 1 < lengths[:, None]).astype(jnp.float32)
    following = from_behind(values[:, 0], "seq", -1)
    next_values = jnp.concatenate([values[:, 1:], following[:, None]], 1)
    delta = (rewards * reward_mask.astype(jnp.float32) + next_valid * next_values - values) * valid
    log_decay = -1.0 / horizon
    offsets = jnp.arange(block, dtype=jnp.int32)
    distance = (offsets[None, :] - offsets[:, None]).astype(jnp.float32)
    upper_mask = distance >= 0.0
    powers = jnp.where(
        upper_mask[None], jnp.exp(jnp.maximum(distance, 0.0)[None] * log_decay[:, None, None]), 0.0
    )
    local_gae = jnp.einsum("rtk,rk->rt", powers, delta, precision=lax.Precision.HIGHEST)
    tail_decay = jnp.exp((block - offsets).astype(jnp.float32)[None, :] * log_decay[:, None])
    start_value = local_gae[:, 0]
    block_decay = jnp.exp(block * log_decay)

    def compose(earlier, later):
        return (later[0] + later[1] * earlier[0], later[1] * earlier[1])

    carry_in, _ = entering(
        (start_value, block_decay),
        "seq",
        compose,
        (jnp.zeros_like(start_value), jnp.ones_like(block_decay)),
    )
    gae = local_gae + tail_decay * carry_in[:, None]
    returns = (gae + values) * valid
    count, first, second = lax.psum(
        (jnp.sum(valid), jnp.sum(gae), jnp.sum(gae * gae)), ("seq", "batch")
    )
    mean = first / count
    var = jnp.maximum(second / count - mean * mean, 1.0)
    whitened = (gae - mean) * valid * lax.rsqrt(var)
    out_adv, out_returns = (
        lax.all_to_all(whitened, "batch", split_axis=1, concat_axis=0, tiled=True),
        lax.all_to_all(returns, "batch", split_axis=1, concat_axis=0, tiled=True),
    )
    return (out_adv, out_returns)


def solution(mesh):
    return jax.shard_map(
        per_device,
        mesh=mesh,
        in_specs=(
            P("batch", None, "seq"),
            P("seq"),
            P("seq"),
            P("batch", "seq"),
            P("batch", "seq"),
            P("batch"),
            P("batch"),
        ),
        out_specs=(P(None, ("seq", "batch")), P(None, ("seq", "batch"))),
        check_vma=False,
    )
```

profile of v0, /device:TPU:10, one launch (start us, length us, event | category | flops | bytes accessed | tf_op | source)
XLA Modules:
  0.0 239.2 jit_solution(13834046668706539538)
XLA Ops:
  7.2 0.7 mul.99
  7.9 3.7 %fusion.2 = (f32[2,2048]{1,0:T(2,128)S(1)}, f32[2,2048]{1,0:T(2,128)S(1)}) fusion(bf16[2,2048,512]{2,1,0:T(8,128)(2,1)} %param.9, f32[512]{0:T(512)S(1)} %mul.99), kind=kLoop, calls=%fused_computation.7 | loop fusion | flops 10477568 | bytes 4229120 | tf_op jit(solution)/shard_map/reduce_sum | solution.py:38
  11.7 1.4 copy.23
  13.1 1.4 copy.25
  16.1 62.7 %reduce-scatter.7.cloned.1.call-done = f32[256,2]{1,0:T(8,128)} async-done(((f32[2048,2]{1,0:T(8,128)}), f32[256,2]{1,0:T(8,128)}) %reduce-scatter.7.cloned.1.call-update) | async-done | bytes 2064
  78.7 1.0 copy.24
  79.7 65.6 %reduce-scatter.9.cloned.1.call-done = f32[256,2]{1,0:T(8,128)} async-done(((f32[2048,2]{1,0:T(8,128)}), f32[256,2]{1,0:T(8,128)}) %reduce-scatter.9.cloned.1.call-update) | async-done | bytes 2064
  145.3 1.0 copy.26
  146.5 2.5 %collective-permute-start = (f32[2]{0:T(128)S(1)}, f32[2]{0:T(128)S(1)}, u32[]{:S(2)}, u32[]{:S(2)}) collective-permute-start(f32[2]{0:T(128)S(1)} %slice_reduce_fusion.1), channel_id=1, source_target_pairs={{4,0},{8,4},{12,8},{16,12},{20,16},{24,20},{28,24},{5,1},{9,5},{13... | collective-permute-start | bytes 32 | tf_op jit(solution)/shard_map/ppermute | solution.py:13
  148.9 3.9 %collective-permute-done = f32[2]{0:T(128)S(1)} collective-permute-done((f32[2]{0:T(128)S(1)}, f32[2]{0:T(128)S(1)}, u32[]{:S(2)}, u32[]{:S(2)}) %collective-permute-start) | collective-permute-done | bytes 40 | tf_op jit(solution)/shard_map/ppermute | solution.py:13
  153.0 0.7 fusion.3
  154.1 14.3 %all-reduce.3 = (f32[16]{0:T(128)S(1)}, f32[16]{0:T(128)S(1)}) all-reduce(f32[16]{0:T(128)S(1)} %dynamic-update-slice, f32[16]{0:T(128)S(1)} %get-tuple-element.174), channel_id=2, replica_groups=mesh['seq'=8,'batch'=4] {'seq'}, use_global_device_ids=true, to_apply=%add | all-reduce | flops 32 | bytes 256
  168.9 0.7 compare_select_fusion
  169.5 0.7 fusion.18
  170.2 43.4 %all-reduce.2 = (f32[]{:T(128)}, f32[]{:T(128)}, f32[]{:T(128)}) all-reduce(f32[]{:T(128)} %get-tuple-element.156, f32[]{:T(128)} %get-tuple-element.176, f32[]{:T(128)} %get-tuple-element.155), channel_id=1, replica_groups=mesh['seq'=8,'batch'=4] {'seq','batch'}, use_global_device_ids=true, to_apply=%region_11.12 | all-reduce | flops 3 | bytes 24 | tf_op jit(solution)/shard_map/psum | solution.py:74
  217.1 3.2 %all-to-all-start = ((f32[4,1,128]{2,1,0:T(1,128)}), f32[4,1,128]{2,1,0:T(1,128)S(1)}, u32[]{:S(2)}, u32[]{:S(2)}) async-start(f32[4,1,128]{2,1,0:T(1,128)} %reshape.73), calls=%async_computation | async-start | bytes 4096 | tf_op jit(solution)/shard_map/all_to_all | solution.py:81
  220.4 0.7 reshape.75
  221.1 2.9 %all-to-all-done = f32[4,1,128]{2,1,0:T(1,128)S(1)} async-done(((f32[4,1,128]{2,1,0:T(1,128)}), f32[4,1,128]{2,1,0:T(1,128)S(1)}, u32[]{:S(2)}, u32[]{:S(2)}) %all-to-all-start) | async-done | bytes 2080 | tf_op jit(solution)/shard_map/all_to_all | solution.py:81
  224.0 3.2 %all-to-all-start.1 = ((f32[4,1,128]{2,1,0:T(1,128)}), f32[4,1,128]{2,1,0:T(1,128)S(1)}, u32[]{:S(2)}, u32[]{:S(2)}) async-start(f32[4,1,128]{2,1,0:T(1,128)} %reshape.75), calls=%async_computation.1 | async-start | bytes 4096 | tf_op jit(solution)/shard_map/all_to_all | solution.py:82
  227.8 0.7 reduce.4
  228.4 0.7 reshape.74
  229.1 1.9 all-to-all-done.1
  231.0 0.7 reduce.5
  231.7 0.7 reshape.76
  (49 shorter events, 3.8 us)
Async XLA Ops:
  7.2 71.6 %reduce-scatter.7.cloned.1.call-start = ((), (), s32[]{:S(2)}) async-start(), calls=%async_computation.4 | async-start | bytes 1179648
  7.9 6.8 %copy-start.4 = (u32[32]{0:T(128)S(1)}, u32[32]{0:T(128)}, u32[]{:S(2)}) copy-start(u32[32]{0:T(128)} %constant.81) | copy-start | bytes 388
  7.9 8.0 %copy-start.3 = (f32[2]{0:T(128)S(1)}, f32[2]{0:T(128)}, u32[]{:S(2)}) copy-start(f32[2]{0:T(128)} %param.15) | copy-start | bytes 28
  7.9 145.0 %copy-start = (s32[2]{0:T(128)S(1)}, s32[2]{0:T(128)}, u32[]{:S(2)}) copy-start(s32[2]{0:T(128)} %param.14) | copy-start | bytes 28
  7.9 145.0 %copy-start.1 = (f32[2,256]{1,0:T(2,128)S(1)}, f32[2,256]{1,0:T(2,128)}, u32[]{:S(2)}) copy-start(f32[2,256]{1,0:T(2,128)} %param.12) | copy-start | bytes 6148
  7.9 145.0 %copy-start.2 = (s32[2,256]{1,0:T(2,128)S(1)}, s32[2,256]{1,0:T(2,128)}, u32[]{:S(2)}) copy-start(s32[2,256]{1,0:T(2,128)} %param.13) | copy-start | bytes 6148
  13.1 132.2 %reduce-scatter.9.cloned.1.call-start = ((), (), s32[]{:S(2)}) async-start(), calls=%async_computation.5 | async-start | bytes 1179648
  146.5 6.4 %collective-permute-start = (f32[2]{0:T(128)S(1)}, f32[2]{0:T(128)S(1)}, u32[]{:S(2)}, u32[]{:S(2)}) collective-permute-start(f32[2]{0:T(128)S(1)} %slice_reduce_fusion.1), channel_id=1, source_target_pairs={{4,0},{8,4},{12,8},{16,12},{20,16},{24,20},{28,24},{5,1},{9,5},{13... | collective-permute-start | bytes 32 | tf_op jit(solution)/shard_map/ppermute | solution.py:13
  217.1 6.9 %all-to-all-start = ((f32[4,1,128]{2,1,0:T(1,128)}), f32[4,1,128]{2,1,0:T(1,128)S(1)}, u32[]{:S(2)}, u32[]{:S(2)}) async-start(f32[4,1,128]{2,1,0:T(1,128)} %reshape.73), calls=%async_computation | async-start | bytes 4096 | tf_op jit(solution)/shard_map/all_to_all | solution.py:81
  224.0 7.0 %all-to-all-start.1 = ((f32[4,1,128]{2,1,0:T(1,128)}), f32[4,1,128]{2,1,0:T(1,128)S(1)}, u32[]{:S(2)}, u32[]{:S(2)}) async-start(f32[4,1,128]{2,1,0:T(1,128)} %reshape.75), calls=%async_computation.1 | async-start | bytes 4096 | tf_op jit(solution)/shard_map/all_to_all | solution.py:82
Sparse Core Ops, SparseCore 0:
  13.2 65.5 reduce-scatter.6
  82.2 63.0 reduce-scatter.8
where the time goes:
time: 240 us; the launch traced here: 239 us
  waiting for transfers between devices  137 us (57%)
  blocking collectives  57.7 us (24%)
  between operations  17.5 us (7%)
  local copies, waits for them, and re-layouts  9.54 us (4%)
  starting transfers between devices  9.02 us (4%)
  other arithmetic  7.63 us (3%)
    unnamed x4, waiting for transfers between devices  128 us
    psum x1, blocking collectives, per_device(): lax.psum((jnp.sum(valid), jnp.sum(gae), jnp.sum(gae * gae)), ('seq', 'bat...  43.4 us
    unnamed x1, blocking collectives  14.3 us
    unnamed x22, local copies, waits for them, and re-layouts  8.28 us
  transfers between devices with their start and end apart: 5, of which 5 were waited for; matrix products, arithmetic and copies ran while one was open for 2% of the time, Pallas kernels for 0%

commit v1 on v0

--- a/solution.py
+++ b/solution.py
@@ -72,7 +72,7 @@
     gae = local_gae + tail_decay * carry_in[:, None]
     returns = (gae + values) * valid
     count, first, second = lax.psum(
-        (jnp.sum(valid), jnp.sum(gae), jnp.sum(gae * gae)), ("seq", "batch")
+        lax.psum((jnp.sum(valid), jnp.sum(gae), jnp.sum(gae * gae)), "batch"), "seq"
     )
     mean = first / count
     var = jnp.maximum(second / count - mean * mean, 1.0)

time: 240 us -> 226 us (0.942); the launches traced: 239 us -> 222 us
  blocking collectives: 57.7 us -> 40.3 us
    psum x1 -> x2, blocking collectives: 43.4 us -> 26.1 us  [the longest x1 19.7 us: per_device(): lax.psum(lax.psum((jnp.sum(valid), jnp.sum(gae), jnp.sum(gae * gae)), 'ba...]
  transfers between devices with their start and end apart: 5 -> 5, of which waited for: 5 -> 5; matrix products, arithmetic and copies ran while one was open for 2% -> 3% of each run, Pallas kernels for 0% -> 0%
where the time goes in v1:
time: 226 us; the launch traced here: 222 us
  waiting for transfers between devices  137 us (61%)
  blocking collectives  40.3 us (18%)
  between operations  17.5 us (8%)
  local copies, waits for them, and re-layouts  9.54 us (4%)
  starting transfers between devices  9.02 us (4%)
  other arithmetic  7.55 us (3%)
    unnamed x4, waiting for transfers between devices  128 us
    psum x1, blocking collectives, per_device(): lax.psum(lax.psum((jnp.sum(valid), jnp.sum(gae), jnp.sum(gae * gae)), 'ba...  19.7 us
    unnamed x1, blocking collectives  14.3 us
    unnamed x22, local copies, waits for them, and re-layouts  8.28 us
    psum x1, blocking collectives, per_device(): lax.psum((jnp.sum(valid), jnp.sum(gae), jnp.sum(gae * gae)), 'batch')  6.35 us
  transfers between devices with their start and end apart: 5, of which 5 were waited for; matrix products, arithmetic and copies ran while one was open for 3% of the time, Pallas kernels for 0%

profile of v1, /device:TPU:10, one launch (start us, length us, event | category | flops | bytes accessed | tf_op | source)
XLA Modules:
  0.0 221.7 jit_solution(16959910384667161370)
XLA Ops:
  7.2 0.7 mul.99
  7.9 3.7 %fusion.2 = (f32[2,2048]{1,0:T(2,128)S(1)}, f32[2,2048]{1,0:T(2,128)S(1)}) fusion(bf16[2,2048,512]{2,1,0:T(8,128)(2,1)} %param.9, f32[512]{0:T(512)S(1)} %mul.99), kind=kLoop, calls=%fused_computation.7 | loop fusion | flops 10477568 | bytes 4229120 | tf_op jit(solution)/shard_map/reduce_sum | solution.py:38
  11.7 1.4 copy.23
  13.1 1.4 copy.25
  16.1 62.7 %reduce-scatter.7.cloned.1.call-done = f32[256,2]{1,0:T(8,128)} async-done(((f32[2048,2]{1,0:T(8,128)}), f32[256,2]{1,0:T(8,128)}) %reduce-scatter.7.cloned.1.call-update) | async-done | bytes 2064
  78.7 1.0 copy.24
  79.7 65.6 %reduce-scatter.9.cloned.1.call-done = f32[256,2]{1,0:T(8,128)} async-done(((f32[2048,2]{1,0:T(8,128)}), f32[256,2]{1,0:T(8,128)}) %reduce-scatter.9.cloned.1.call-update) | async-done | bytes 2064
  145.3 1.0 copy.26
  146.5 2.5 %collective-permute-start = (f32[2]{0:T(128)S(1)}, f32[2]{0:T(128)S(1)}, u32[]{:S(2)}, u32[]{:S(2)}) collective-permute-start(f32[2]{0:T(128)S(1)} %slice_reduce_fusion.1), channel_id=1, source_target_pairs={{4,0},{8,4},{12,8},{16,12},{20,16},{24,20},{28,24},{5,1},{9,5},{13... | collective-permute-start | bytes 32 | tf_op jit(solution)/shard_map/ppermute | solution.py:13
  148.9 3.9 %collective-permute-done = f32[2]{0:T(128)S(1)} collective-permute-done((f32[2]{0:T(128)S(1)}, f32[2]{0:T(128)S(1)}, u32[]{:S(2)}, u32[]{:S(2)}) %collective-permute-start) | collective-permute-done | bytes 40 | tf_op jit(solution)/shard_map/ppermute | solution.py:13
  153.0 0.7 fusion.3
  154.1 14.3 %all-reduce.3 = (f32[16]{0:T(128)S(1)}, f32[16]{0:T(128)S(1)}) all-reduce(f32[16]{0:T(128)S(1)} %dynamic-update-slice, f32[16]{0:T(128)S(1)} %get-tuple-element.177), channel_id=2, replica_groups=mesh['seq'=8,'batch'=4] {'seq'}, use_global_device_ids=true, to_apply=%add | all-reduce | flops 32 | bytes 256
  168.9 0.7 compare_select_fusion
  170.1 6.3 %all-reduce.4 = (f32[]{:T(128)}, f32[]{:T(128)}, f32[]{:T(128)}) all-reduce(f32[]{:T(128)} %get-tuple-element.156, f32[]{:T(128)} %get-tuple-element.179, f32[]{:T(128)} %get-tuple-element.155), channel_id=1, replica_groups=mesh['seq'=8,'batch'=4] {'batch'}, use_global_device_ids=true, to_apply=%region_13.14 | all-reduce | flops 3 | bytes 24 | tf_op jit(solution)/shard_map/psum | solution.py:75
  176.5 19.7 %all-reduce.2 = (f32[]{:T(128)}, f32[]{:T(128)}, f32[]{:T(128)}) all-reduce(f32[]{:T(128)} %get-tuple-element.172, f32[]{:T(128)} %get-tuple-element.173, f32[]{:T(128)} %get-tuple-element.174), channel_id=1, replica_groups=mesh['seq'=8,'batch'=4] {'seq'}, use_global_device_ids=true, to_apply=%region_14.15 | all-reduce | flops 3 | bytes 24 | tf_op jit(solution)/shard_map/psum | solution.py:74
  199.7 3.2 %all-to-all-start = ((f32[4,1,128]{2,1,0:T(1,128)}), f32[4,1,128]{2,1,0:T(1,128)S(1)}, u32[]{:S(2)}, u32[]{:S(2)}) async-start(f32[4,1,128]{2,1,0:T(1,128)} %reshape.73), calls=%async_computation | async-start | bytes 4096 | tf_op jit(solution)/shard_map/all_to_all | solution.py:81
  203.0 0.7 reshape.75
  203.7 2.9 %all-to-all-done = f32[4,1,128]{2,1,0:T(1,128)S(1)} async-done(((f32[4,1,128]{2,1,0:T(1,128)}), f32[4,1,128]{2,1,0:T(1,128)S(1)}, u32[]{:S(2)}, u32[]{:S(2)}) %all-to-all-start) | async-done | bytes 2080 | tf_op jit(solution)/shard_map/all_to_all | solution.py:81
  206.6 3.2 %all-to-all-start.1 = ((f32[4,1,128]{2,1,0:T(1,128)}), f32[4,1,128]{2,1,0:T(1,128)S(1)}, u32[]{:S(2)}, u32[]{:S(2)}) async-start(f32[4,1,128]{2,1,0:T(1,128)} %reshape.75), calls=%async_computation.1 | async-start | bytes 4096 | tf_op jit(solution)/shard_map/all_to_all | solution.py:82
  210.3 0.7 reduce.4
  211.0 0.7 reshape.74
  211.7 1.9 all-to-all-done.1
  213.6 0.7 reduce.5
  214.2 0.7 reshape.76
  (50 shorter events, 4.4 us)
Async XLA Ops:
  7.2 71.6 %reduce-scatter.7.cloned.1.call-start = ((), (), s32[]{:S(2)}) async-start(), calls=%async_computation.4 | async-start | bytes 1179648
  7.9 6.8 %copy-start.4 = (u32[32]{0:T(128)S(1)}, u32[32]{0:T(128)}, u32[]{:S(2)}) copy-start(u32[32]{0:T(128)} %constant.81) | copy-start | bytes 388
  7.9 8.0 %copy-start.3 = (f32[2]{0:T(128)S(1)}, f32[2]{0:T(128)}, u32[]{:S(2)}) copy-start(f32[2]{0:T(128)} %param.15) | copy-start | bytes 28
  7.9 145.0 %copy-start = (s32[2]{0:T(128)S(1)}, s32[2]{0:T(128)}, u32[]{:S(2)}) copy-start(s32[2]{0:T(128)} %param.14) | copy-start | bytes 28
  7.9 145.0 %copy-start.1 = (f32[2,256]{1,0:T(2,128)S(1)}, f32[2,256]{1,0:T(2,128)}, u32[]{:S(2)}) copy-start(f32[2,256]{1,0:T(2,128)} %param.12) | copy-start | bytes 6148
  7.9 145.0 %copy-start.2 = (s32[2,256]{1,0:T(2,128)S(1)}, s32[2,256]{1,0:T(2,128)}, u32[]{:S(2)}) copy-start(s32[2,256]{1,0:T(2,128)} %param.13) | copy-start | bytes 6148
  13.1 132.2 %reduce-scatter.9.cloned.1.call-start = ((), (), s32[]{:S(2)}) async-start(), calls=%async_computation.5 | async-start | bytes 1179648
  146.5 6.4 %collective-permute-start = (f32[2]{0:T(128)S(1)}, f32[2]{0:T(128)S(1)}, u32[]{:S(2)}, u32[]{:S(2)}) collective-permute-start(f32[2]{0:T(128)S(1)} %slice_reduce_fusion.1), channel_id=1, source_target_pairs={{4,0},{8,4},{12,8},{16,12},{20,16},{24,20},{28,24},{5,1},{9,5},{13... | collective-permute-start | bytes 32 | tf_op jit(solution)/shard_map/ppermute | solution.py:13
  199.7 6.9 %all-to-all-start = ((f32[4,1,128]{2,1,0:T(1,128)}), f32[4,1,128]{2,1,0:T(1,128)S(1)}, u32[]{:S(2)}, u32[]{:S(2)}) async-start(f32[4,1,128]{2,1,0:T(1,128)} %reshape.73), calls=%async_computation | async-start | bytes 4096 | tf_op jit(solution)/shard_map/all_to_all | solution.py:81
  206.6 7.0 %all-to-all-start.1 = ((f32[4,1,128]{2,1,0:T(1,128)}), f32[4,1,128]{2,1,0:T(1,128)S(1)}, u32[]{:S(2)}, u32[]{:S(2)}) async-start(f32[4,1,128]{2,1,0:T(1,128)} %reshape.75), calls=%async_computation.1 | async-start | bytes 4096 | tf_op jit(solution)/shard_map/all_to_all | solution.py:82
Sparse Core Ops, SparseCore 0:
  13.2 65.5 reduce-scatter.6
  82.2 63.0 reduce-scatter.8
